TPU v7x, 256 devices: a whole 4x4x8 slice. The times are simulated.
256 devices in a mesh: tm: 64 (over z_lo, y, x, core), space: 4 (over z_hi).
Axes of the slice: x: 4, y: 4, z: 8 (z_hi: 4, z_lo: 2; z = z_hi * 2 + z_lo), core: 2. Of those that a mesh axis runs over, the one named last changes fastest.
Arguments:
- rhs: float32 [128, 1024, 1024], P('tm', 'space'), may hold values from -6 to 6
- guess: float32 [128, 1024, 1024], P('tm', 'space'), may hold values from -6 to 6
- diffusion: float32 [1024, 1024], P('space'), may hold values from 0.2 to 2
Outputs:
- solution: float32 [128, 1024, 1024], P('tm', 'space')
- norms: float32 [6], replicated
All inputs are finite; a program needn't handle non-finite values.
Results may differ from a plain program's by a relative error of at most 0.0001.
Values sent between devices are 32-bit elements; how exact they have to be, the bound alone decides.
A program may use at most 64 MiB of HBM per device.

v0:
```python
import jax
import jax.numpy as jnp
from jax import lax
from jax.sharding import Mesh
from jax.sharding import PartitionSpec as P

LEVELS = 5
TM = ("tm_0", "tm_1", "tm_2", "tm_3")
TM_SPACE = ("tm_0", "tm_1", "tm_2", "tm_3", "space")


damping = 0.8


def with_halo(block, sides, width):
    for axis, dim in sides:
        count = lax.axis_size(axis)
        forward = [(i, i + 1) for i in range(count - 1)]
        backward = [(target, source) for source, target in forward]
        low = lax.ppermute(
            lax.slice_in_dim(block, block.shape[dim] - width, None, axis=dim), axis, forward
        )
        high = lax.ppermute(lax.slice_in_dim(block, 0, width, axis=dim), axis, backward)
        block = jnp.concatenate([low, block, high], axis=dim)
    return block


def shifted(value, axis, steps):
    count = lax.axis_size(axis)
    first, last = (max(0, -steps), min(count, count - steps))
    return lax.ppermute(value, axis, [(source, source + steps) for source in range(first, last)])


def from_partner(value, axis, apart):
    mask = 2**apart
    pairs = [(source, source ^ mask) for source in range(lax.axis_size(axis))]
    return lax.ppermute(value, axis, pairs)


def over_axes(array, axes):
    for axis in axes:
        array = lax.psum(array, axis)
    return array


def neighbours(field):
    rows = with_halo(field, (("space", 1),), 1)
    padded = jnp.pad(rows, ((0, 0), (0, 0), (1, 1)))
    total = padded[:, 2:, 1:-1] + padded[:, :-2, 1:-1]
    total = total + padded[:, 1:-1, 2:] + padded[:, 1:-1, :-2]
    return total


def residual(field, source, scaled, diag, stride):
    earlier = shifted(field[-1:], TM, stride)
    before = jnp.concatenate([earlier, field[:-1]], axis=0)
    image = diag * field - scaled * neighbours(field) - before
    return source - image


def stride_of(level):
    if level == 0:
        return 1
    return 2 ** (level - 1)


def body(rhs, guess, diffusion):
    position = lax.axis_index(TM)
    cells = rhs.shape[1] * lax.axis_size("space") * rhs.shape[2]
    partials = []

    def weight_of(level):
        if level <= 1:
            return jnp.float32(1.0)
        stride = stride_of(level)
        return jnp.where(position % stride == stride - 1, 1.0, 0.0).astype(jnp.float32)

    def record(resid, level):
        local_part = jnp.sum(resid * resid) * weight_of(level)
        partials.append(local_part)

    sources = [rhs]
    fields = []
    field = guess
    for level in range(LEVELS - 1):
        source = sources[level]
        scaled = 2.0**level * diffusion
        diag = 1.0 + 4.0 * scaled
        stride = stride_of(level)
        if level == 0:
            field = field + damping * residual(field, source, scaled, diag, stride) / diag
        else:
            field = damping * source / diag
        resid = residual(field, source, scaled, diag, stride)
        record(resid, level)
        fields.append(field)
        if level == 0:
            coarse = resid[0:1] + resid[1:2]
        else:
            coarse = resid + from_partner(resid, TM, level - 1)
        sources.append(coarse)
    level = LEVELS - 1
    source = sources[level]
    scaled = 2.0**level * diffusion
    diag = 1.0 + 4.0 * scaled
    stride = stride_of(level)
    field = damping * source / diag
    field = field + damping * residual(field, source, scaled, diag, stride) / diag
    resid = residual(field, source, scaled, diag, stride)
    record(resid, level)
    correction = field
    for level in range(LEVELS - 2, -1, -1):
        scaled = 2.0**level * diffusion
        diag = 1.0 + 4.0 * scaled
        stride = stride_of(level)
        field = fields[level] + correction
        field = field + damping * residual(field, sources[level], scaled, diag, stride) / diag
        correction = field
    scaled = 1.0 * diffusion
    diag = 1.0 + 4.0 * scaled
    resid = residual(correction, rhs, scaled, diag, 1)
    record(resid, 0)
    totals = over_axes(jnp.stack(partials), TM_SPACE)
    norms = jnp.sqrt(totals / cells)
    return (correction, norms)


def solution(mesh):
    split = Mesh(
        mesh.devices.reshape(2, 4, 4, 2, mesh.shape["space"]),
        ("tm_0", "tm_1", "tm_2", "tm_3", "space"),
    )
    return jax.shard_map(
        body,
        mesh=split,
        in_specs=(P(TM, "space", None), P(TM, "space", None), P("space", None)),
        out_specs=(P(TM, "space", None), P()),
        check_vma=False,
    )
```

profile of v0, /device:TPU:1, one launch (start us, length us, event | category | flops | bytes accessed | tf_op | source)
XLA Modules:
  0.0 390.7 jit_solution(6274208808980267438)
XLA Ops:
  2.5 4.5 %collective-permute-start.2 = (f32[1,256,1024]{2,1,0:T(8,128)S(1)}, f32[1,256,1024]{2,1,0:T(8,128)S(1)}, u32[]{:S(2)}, u32[]{:S(2)}) collective-permute-start(f32[1,256,1024]{2,1,0:T(8,128)S(1)} %get-tuple-element.30), channel_id=1, source_target_pairs={{0,4},{4,8},{8,12},{12,16},{16,20},{20,24},{24,28},{28,32},{32,36}... | collective-permute-start | bytes 3145736 | tf_op jit(solution)/shard_map/ppermute | solution.py:31
  8.4 5.5 %collective-permute-start.1 = (f32[2,1,1024]{2,1,0:T(1,128)S(1)}, f32[2,1,1024]{2,1,0:T(1,128)S(1)}, u32[]{:S(2)}, u32[]{:S(2)}) collective-permute-start(f32[2,1,1024]{2,1,0:T(1,128)S(1)} %get-tuple-element.32), channel_id=1, source_target_pairs={{0,1},{1,2},{2,3},{4,5},{5,6},{6,7},{8,9},{9,10},{10,11},{12,13},{... | collective-permute-start | bytes 24584 | tf_op jit(solution)/shard_map/ppermute | solution.py:20
  20.8 4.4 %collective-permute-start.5 = (f32[1,256,1024]{2,1,0:T(8,128)S(1)}, f32[1,256,1024]{2,1,0:T(8,128)S(1)}, u32[]{:S(2)}, u32[]{:S(2)}) collective-permute-start(f32[1,256,1024]{2,1,0:T(8,128)S(1)} %get-tuple-element.28), channel_id=1, source_target_pairs={{0,4},{4,8},{8,12},{12,16},{16,20},{20,24},{24,28},{28,32},{32,36}... | collective-permute-start | bytes 3145736 | tf_op jit(solution)/shard_map/ppermute | solution.py:31
  26.5 5.5 %collective-permute-start.4 = (f32[2,1,1024]{2,1,0:T(1,128)S(1)}, f32[2,1,1024]{2,1,0:T(1,128)S(1)}, u32[]{:S(2)}, u32[]{:S(2)}) collective-permute-start(f32[2,1,1024]{2,1,0:T(1,128)S(1)} %get-tuple-element.26), channel_id=1, source_target_pairs={{0,1},{1,2},{2,3},{4,5},{5,6},{6,7},{8,9},{9,10},{10,11},{12,13},{... | collective-permute-start | bytes 24584 | tf_op jit(solution)/shard_map/ppermute | solution.py:20
  39.6 4.4 %collective-permute-start.8 = (f32[1,256,1024]{2,1,0:T(8,128)S(1)}, f32[1,256,1024]{2,1,0:T(8,128)S(1)}, u32[]{:S(2)}, u32[]{:S(2)}) collective-permute-start(f32[1,256,1024]{2,1,0:T(8,128)S(1)} %bitcast_divide_fusion.3), channel_id=1, source_target_pairs={{0,4},{4,8},{8,12},{12,16},{16,20},{20,24},{24,28},{28,32},{32,36}... | collective-permute-start | bytes 3145736 | tf_op jit(solution)/shard_map/ppermute | solution.py:31
  45.3 5.5 %collective-permute-start.7 = (f32[1,1,1024]{2,1,0:T(1,128)S(1)}, f32[1,1,1024]{2,1,0:T(1,128)S(1)}, u32[]{:S(2)}, u32[]{:S(2)}) collective-permute-start(f32[1,1,1024]{2,1,0:T(1,128)S(1)} %get-tuple-element.48), channel_id=1, source_target_pairs={{0,1},{1,2},{2,3},{4,5},{5,6},{6,7},{8,9},{9,10},{10,11},{12,13},{... | collective-permute-start | bytes 12296 | tf_op jit(solution)/shard_map/ppermute | solution.py:20
  65.8 5.5 %collective-permute-start.11 = (f32[1,1,1024]{2,1,0:T(1,128)S(1)}, f32[1,1,1024]{2,1,0:T(1,128)S(1)}, u32[]{:S(2)}, u32[]{:S(2)}) collective-permute-start(f32[1,1,1024]{2,1,0:T(1,128)S(1)} %get-tuple-element.46), channel_id=1, source_target_pairs={{0,1},{1,2},{2,3},{4,5},{5,6},{6,7},{8,9},{9,10},{10,11},{12,13},{... | collective-permute-start | bytes 12296 | tf_op jit(solution)/shard_map/ppermute | solution.py:20
  72.5 14.1 %collective-permute-done.12 = f32[1,256,1024]{2,1,0:T(8,128)S(1)} collective-permute-done((f32[1,256,1024]{2,1,0:T(8,128)S(1)}, f32[1,256,1024]{2,1,0:T(8,128)S(1)}, u32[]{:S(2)}, u32[]{:S(2)}) %collective-permute-start.12) | collective-permute-done | bytes 1048608 | tf_op jit(solution)/shard_map/ppermute | solution.py:31
  90.2 22.3 %collective-permute-done.13 = f32[1,256,1024]{2,1,0:T(8,128)S(1)} collective-permute-done((f32[1,256,1024]{2,1,0:T(8,128)S(1)}, f32[1,256,1024]{2,1,0:T(8,128)S(1)}, u32[]{:S(2)}, u32[]{:S(2)}) %collective-permute-start.13) | collective-permute-done | bytes 1048608 | tf_op jit(solution)/shard_map/ppermute | solution.py:37
  112.9 9.8 %collective-permute-start.16 = (f32[1,256,1024]{2,1,0:T(8,128)S(1)}, f32[1,256,1024]{2,1,0:T(8,128)S(1)}, u32[]{:S(2)}, u32[]{:S(2)}) collective-permute-start(f32[1,256,1024]{2,1,0:T(8,128)S(1)} %get-tuple-element.14), channel_id=1, source_target_pairs={{0,16},{4,20},{8,24},{12,28},{16,32},{20,36},{24,40},{28,44},{32,4... | collective-permute-start | bytes 3145736 | tf_op jit(solution)/shard_map/ppermute | solution.py:31
  124.0 5.5 %collective-permute-start.15 = (f32[1,1,1024]{2,1,0:T(1,128)S(1)}, f32[1,1,1024]{2,1,0:T(1,128)S(1)}, u32[]{:S(2)}, u32[]{:S(2)}) collective-permute-start(f32[1,1,1024]{2,1,0:T(1,128)S(1)} %get-tuple-element.44), channel_id=1, source_target_pairs={{0,1},{1,2},{2,3},{4,5},{5,6},{6,7},{8,9},{9,10},{10,11},{12,13},{... | collective-permute-start | bytes 12296 | tf_op jit(solution)/shard_map/ppermute | solution.py:20
  130.7 12.6 %collective-permute-done.16 = f32[1,256,1024]{2,1,0:T(8,128)S(1)} collective-permute-done((f32[1,256,1024]{2,1,0:T(8,128)S(1)}, f32[1,256,1024]{2,1,0:T(8,128)S(1)}, u32[]{:S(2)}, u32[]{:S(2)}) %collective-permute-start.16) | collective-permute-done | bytes 1048608 | tf_op jit(solution)/shard_map/ppermute | solution.py:31
  149.1 21.2 %collective-permute-done.17 = f32[1,256,1024]{2,1,0:T(8,128)S(1)} collective-permute-done((f32[1,256,1024]{2,1,0:T(8,128)S(1)}, f32[1,256,1024]{2,1,0:T(8,128)S(1)}, u32[]{:S(2)}, u32[]{:S(2)}) %collective-permute-start.17) | collective-permute-done | bytes 1048608 | tf_op jit(solution)/shard_map/ppermute | solution.py:37
  170.7 5.4 %collective-permute-start.20 = (f32[1,256,1024]{2,1,0:T(8,128)S(1)}, f32[1,256,1024]{2,1,0:T(8,128)S(1)}, u32[]{:S(2)}, u32[]{:S(2)}) collective-permute-start(f32[1,256,1024]{2,1,0:T(8,128)S(1)} %get-tuple-element.12), channel_id=1, source_target_pairs={{0,32},{4,36},{8,40},{12,44},{16,48},{20,52},{24,56},{28,60},{32,6... | collective-permute-start | bytes 3145736 | tf_op jit(solution)/shard_map/ppermute | solution.py:31
  177.4 5.5 %collective-permute-start.19 = (f32[1,1,1024]{2,1,0:T(1,128)S(1)}, f32[1,1,1024]{2,1,0:T(1,128)S(1)}, u32[]{:S(2)}, u32[]{:S(2)}) collective-permute-start(f32[1,1,1024]{2,1,0:T(1,128)S(1)} %get-tuple-element.42), channel_id=1, source_target_pairs={{0,1},{1,2},{2,3},{4,5},{5,6},{6,7},{8,9},{9,10},{10,11},{12,13},{... | collective-permute-start | bytes 12296 | tf_op jit(solution)/shard_map/ppermute | solution.py:20
  184.1 10.0 %collective-permute-done.20 = f32[1,256,1024]{2,1,0:T(8,128)S(1)} collective-permute-done((f32[1,256,1024]{2,1,0:T(8,128)S(1)}, f32[1,256,1024]{2,1,0:T(8,128)S(1)}, u32[]{:S(2)}, u32[]{:S(2)}) %collective-permute-start.20) | collective-permute-done | bytes 1048608 | tf_op jit(solution)/shard_map/ppermute | solution.py:31
  199.9 5.5 %collective-permute-start.22 = (f32[1,1,1024]{2,1,0:T(1,128)S(1)}, f32[1,1,1024]{2,1,0:T(1,128)S(1)}, u32[]{:S(2)}, u32[]{:S(2)}) collective-permute-start(f32[1,1,1024]{2,1,0:T(1,128)S(1)} %get-tuple-element.40), channel_id=1, source_target_pairs={{0,1},{1,2},{2,3},{4,5},{5,6},{6,7},{8,9},{9,10},{10,11},{12,13},{... | collective-permute-start | bytes 12296 | tf_op jit(solution)/shard_map/ppermute | solution.py:20
  206.6 9.5 %collective-permute-done.23 = f32[1,256,1024]{2,1,0:T(8,128)S(1)} collective-permute-done((f32[1,256,1024]{2,1,0:T(8,128)S(1)}, f32[1,256,1024]{2,1,0:T(8,128)S(1)}, u32[]{:S(2)}, u32[]{:S(2)}) %collective-permute-start.23) | collective-permute-done | bytes 1048608 | tf_op jit(solution)/shard_map/ppermute | solution.py:31
  222.7 5.5 %collective-permute-start.25 = (f32[1,1,1024]{2,1,0:T(1,128)S(1)}, f32[1,1,1024]{2,1,0:T(1,128)S(1)}, u32[]{:S(2)}, u32[]{:S(2)}) collective-permute-start(f32[1,1,1024]{2,1,0:T(1,128)S(1)} %get-tuple-element.38), channel_id=1, source_target_pairs={{0,1},{1,2},{2,3},{4,5},{5,6},{6,7},{8,9},{9,10},{10,11},{12,13},{... | collective-permute-start | bytes 12296 | tf_op jit(solution)/shard_map/ppermute | solution.py:20
  229.4 9.2 %collective-permute-done.26 = f32[1,256,1024]{2,1,0:T(8,128)S(1)} collective-permute-done((f32[1,256,1024]{2,1,0:T(8,128)S(1)}, f32[1,256,1024]{2,1,0:T(8,128)S(1)}, u32[]{:S(2)}, u32[]{:S(2)}) %collective-permute-start.26) | collective-permute-done | bytes 1048608 | tf_op jit(solution)/shard_map/ppermute | solution.py:31
  239.6 10.1 %collective-permute-start.29 = (f32[1,256,1024]{2,1,0:T(8,128)S(1)}, f32[1,256,1024]{2,1,0:T(8,128)S(1)}, u32[]{:S(2)}, u32[]{:S(2)}) collective-permute-start(f32[1,256,1024]{2,1,0:T(8,128)S(1)} %fusion.52), channel_id=1, source_target_pairs={{0,4},{4,8},{8,12},{12,16},{16,20},{20,24},{24,28},{28,32},{32,36}... | collective-permute-start | bytes 3145736 | tf_op jit(solution)/shard_map/ppermute | solution.py:31
  251.0 5.5 %collective-permute-start.28 = (f32[1,1,1024]{2,1,0:T(1,128)S(1)}, f32[1,1,1024]{2,1,0:T(1,128)S(1)}, u32[]{:S(2)}, u32[]{:S(2)}) collective-permute-start(f32[1,1,1024]{2,1,0:T(1,128)S(1)} %get-tuple-element.36), channel_id=1, source_target_pairs={{0,1},{1,2},{2,3},{4,5},{5,6},{6,7},{8,9},{9,10},{10,11},{12,13},{... | collective-permute-start | bytes 12296 | tf_op jit(solution)/shard_map/ppermute | solution.py:20
  264.2 4.4 %collective-permute-start.32 = (f32[1,256,1024]{2,1,0:T(8,128)}, f32[1,256,1024]{2,1,0:T(8,128)}, u32[]{:S(2)}, u32[]{:S(2)}) collective-permute-start(f32[1,256,1024]{2,1,0:T(8,128)} %get-tuple-element.22), channel_id=1, source_target_pairs={{0,4},{4,8},{8,12},{12,16},{16,20},{20,24},{24,28},{28,32},{32,36}... | collective-permute-start | bytes 3145736 | tf_op jit(solution)/shard_map/ppermute | solution.py:31
  271.1 5.5 %collective-permute-start.31 = (f32[2,1,1024]{2,1,0:T(1,128)S(1)}, f32[2,1,1024]{2,1,0:T(1,128)S(1)}, u32[]{:S(2)}, u32[]{:S(2)}) collective-permute-start(f32[2,1,1024]{2,1,0:T(1,128)S(1)} %get-tuple-element.24), channel_id=1, source_target_pairs={{0,1},{1,2},{2,3},{4,5},{5,6},{6,7},{8,9},{9,10},{10,11},{12,13},{... | collective-permute-start | bytes 24584 | tf_op jit(solution)/shard_map/ppermute | solution.py:20
  277.5 9.6 %collective-permute-start.35 = (f32[1,256,1024]{2,1,0:T(8,128)}, f32[1,256,1024]{2,1,0:T(8,128)S(1)}, u32[]{:S(2)}, u32[]{:S(2)}) collective-permute-start(f32[1,256,1024]{2,1,0:T(8,128)} %get-tuple-element.11), channel_id=1, source_target_pairs={{0,32},{4,36},{8,40},{12,44},{16,48},{20,52},{24,56},{28,60},{32,6... | collective-permute-start | bytes 3145736 | tf_op jit(solution)/shard_map/ppermute | solution.py:31
  288.5 6.4 %collective-permute-start.34 = (f32[1,1,1024]{2,1,0:T(1,128)S(1)}, f32[1,1,1024]{2,1,0:T(1,128)S(1)}, u32[]{:S(2)}, u32[]{:S(2)}) collective-permute-start(f32[1,1,1024]{2,1,0:T(1,128)S(1)} %get-tuple-element.34), channel_id=1, source_target_pairs={{0,1},{1,2},{2,3},{4,5},{5,6},{6,7},{8,9},{9,10},{10,11},{12,13},{... | collective-permute-start | bytes 12296 | tf_op jit(solution)/shard_map/ppermute | solution.py:20
  305.2 6.7 %collective-permute-start.37 = (f32[2,1,1024]{2,1,0:T(1,128)S(1)}, f32[2,1,1024]{2,1,0:T(1,128)S(1)}, u32[]{:S(2)}, u32[]{:S(2)}) collective-permute-start(f32[2,1,1024]{2,1,0:T(1,128)S(1)} %get-tuple-element.20), channel_id=1, source_target_pairs={{0,1},{1,2},{2,3},{4,5},{5,6},{6,7},{8,9},{9,10},{10,11},{12,13},{... | collective-permute-start | bytes 24584 | tf_op jit(solution)/shard_map/ppermute | solution.py:20
  323.2 23.1 %psum.35 = f32[6]{0:T(128)S(1)} all-reduce(f32[6]{0:T(128)S(1)} %stack.27), channel_id=1, replica_groups=mesh['tm_0'=2,'tm_1'=4,'tm_2'=4,'tm_3'=2,'space'=4] {'tm_0'}, use_global_device_ids=true, to_apply=%region_6.7 | all-reduce | flops 6 | bytes 48 | tf_op jit(solution)/shard_map/psum | solution.py:42
  346.3 17.9 %psum.36 = f32[6]{0:T(128)S(1)} all-reduce(f32[6]{0:T(128)S(1)} %psum.35), channel_id=1, replica_groups=mesh['tm_0'=2,'tm_1'=4,'tm_2'=4,'tm_3'=2,'space'=4] {'tm_1'}, use_global_device_ids=true, to_apply=%region_7.8 | all-reduce | flops 6 | bytes 48 | tf_op jit(solution)/shard_map/psum | solution.py:42
  364.2 7.6 %psum.37 = f32[6]{0:T(128)S(1)} all-reduce(f32[6]{0:T(128)S(1)} %psum.36), channel_id=1, replica_groups=mesh['tm_0'=2,'tm_1'=4,'tm_2'=4,'tm_3'=2,'space'=4] {'tm_2'}, use_global_device_ids=true, to_apply=%region_8.9 | all-reduce | flops 6 | bytes 48 | tf_op jit(solution)/shard_map/psum | solution.py:42
  371.8 6.5 %psum.38 = f32[6]{0:T(128)S(1)} all-reduce(f32[6]{0:T(128)S(1)} %psum.37), channel_id=1, replica_groups=mesh['tm_0'=2,'tm_1'=4,'tm_2'=4,'tm_3'=2,'space'=4] {'tm_3'}, use_global_device_ids=true, to_apply=%region_9.10 | all-reduce | flops 6 | bytes 48 | tf_op jit(solution)/shard_map/psum | solution.py:42
  378.4 11.8 %psum.39 = f32[6]{0:T(128)S(1)} all-reduce(f32[6]{0:T(128)S(1)} %psum.38), channel_id=1, replica_groups=mesh['tm_0'=2,'tm_1'=4,'tm_2'=4,'tm_3'=2,'space'=4] {'space'}, use_global_device_ids=true, to_apply=%region_10.11 | all-reduce | flops 6 | bytes 48 | tf_op jit(solution)/shard_map/psum | solution.py:42
  (129 shorter events, 100.6 us)
Async XLA Ops:
  2.5 16.2 %collective-permute-start.2 = (f32[1,256,1024]{2,1,0:T(8,128)S(1)}, f32[1,256,1024]{2,1,0:T(8,128)S(1)}, u32[]{:S(2)}, u32[]{:S(2)}) collective-permute-start(f32[1,256,1024]{2,1,0:T(8,128)S(1)} %get-tuple-element.30), channel_id=1, source_target_pairs={{0,4},{4,8},{8,12},{12,16},{16,20},{20,24},{24,28},{28,32},{32,36}... | collective-permute-start | bytes 3145736 | tf_op jit(solution)/shard_map/ppermute | solution.py:31
  7.1 7.0 %collective-permute-start = (f32[2,1,1024]{2,1,0:T(1,128)S(1)}, f32[2,1,1024]{2,1,0:T(1,128)S(1)}, u32[]{:S(2)}, u32[]{:S(2)}) collective-permute-start(f32[2,1,1024]{2,1,0:T(1,128)S(1)} %get-tuple-element.33), channel_id=1, source_target_pairs={{1,0},{2,1},{3,2},{5,4},{6,5},{7,6},{9,8},{10,9},{11,10},{13,12},{... | collective-permute-start | bytes 24584 | tf_op jit(solution)/shard_map/ppermute | solution.py:23
  8.4 6.3 %collective-permute-start.1 = (f32[2,1,1024]{2,1,0:T(1,128)S(1)}, f32[2,1,1024]{2,1,0:T(1,128)S(1)}, u32[]{:S(2)}, u32[]{:S(2)}) collective-permute-start(f32[2,1,1024]{2,1,0:T(1,128)S(1)} %get-tuple-element.32), channel_id=1, source_target_pairs={{0,1},{1,2},{2,3},{4,5},{5,6},{6,7},{8,9},{9,10},{10,11},{12,13},{... | collective-permute-start | bytes 24584 | tf_op jit(solution)/shard_map/ppermute | solution.py:20
  20.8 16.1 %collective-permute-start.5 = (f32[1,256,1024]{2,1,0:T(8,128)S(1)}, f32[1,256,1024]{2,1,0:T(8,128)S(1)}, u32[]{:S(2)}, u32[]{:S(2)}) collective-permute-start(f32[1,256,1024]{2,1,0:T(8,128)S(1)} %get-tuple-element.28), channel_id=1, source_target_pairs={{0,4},{4,8},{8,12},{12,16},{16,20},{20,24},{24,28},{28,32},{32,36}... | collective-permute-start | bytes 3145736 | tf_op jit(solution)/shard_map/ppermute | solution.py:31
  25.2 6.8 %collective-permute-start.3 = (f32[2,1,1024]{2,1,0:T(1,128)S(1)}, f32[2,1,1024]{2,1,0:T(1,128)S(1)}, u32[]{:S(2)}, u32[]{:S(2)}) collective-permute-start(f32[2,1,1024]{2,1,0:T(1,128)S(1)} %get-tuple-element.27), channel_id=1, source_target_pairs={{1,0},{2,1},{3,2},{5,4},{6,5},{7,6},{9,8},{10,9},{11,10},{13,12},{... | collective-permute-start | bytes 24584 | tf_op jit(solution)/shard_map/ppermute | solution.py:23
  26.5 6.3 %collective-permute-start.4 = (f32[2,1,1024]{2,1,0:T(1,128)S(1)}, f32[2,1,1024]{2,1,0:T(1,128)S(1)}, u32[]{:S(2)}, u32[]{:S(2)}) collective-permute-start(f32[2,1,1024]{2,1,0:T(1,128)S(1)} %get-tuple-element.26), channel_id=1, source_target_pairs={{0,1},{1,2},{2,3},{4,5},{5,6},{6,7},{8,9},{9,10},{10,11},{12,13},{... | collective-permute-start | bytes 24584 | tf_op jit(solution)/shard_map/ppermute | solution.py:20
  39.6 16.1 %collective-permute-start.8 = (f32[1,256,1024]{2,1,0:T(8,128)S(1)}, f32[1,256,1024]{2,1,0:T(8,128)S(1)}, u32[]{:S(2)}, u32[]{:S(2)}) collective-permute-start(f32[1,256,1024]{2,1,0:T(8,128)S(1)} %bitcast_divide_fusion.3), channel_id=1, source_target_pairs={{0,4},{4,8},{8,12},{12,16},{16,20},{20,24},{24,28},{28,32},{32,36}... | collective-permute-start | bytes 3145736 | tf_op jit(solution)/shard_map/ppermute | solution.py:31
  44.0 6.8 %collective-permute-start.6 = (f32[1,1,1024]{2,1,0:T(1,128)S(1)}, f32[1,1,1024]{2,1,0:T(1,128)S(1)}, u32[]{:S(2)}, u32[]{:S(2)}) collective-permute-start(f32[1,1,1024]{2,1,0:T(1,128)S(1)} %get-tuple-element.49), channel_id=1, source_target_pairs={{1,0},{2,1},{3,2},{5,4},{6,5},{7,6},{9,8},{10,9},{11,10},{13,12},{... | collective-permute-start | bytes 12296 | tf_op jit(solution)/shard_map/ppermute | solution.py:23
  45.3 6.3 %collective-permute-start.7 = (f32[1,1,1024]{2,1,0:T(1,128)S(1)}, f32[1,1,1024]{2,1,0:T(1,128)S(1)}, u32[]{:S(2)}, u32[]{:S(2)}) collective-permute-start(f32[1,1,1024]{2,1,0:T(1,128)S(1)} %get-tuple-element.48), channel_id=1, source_target_pairs={{0,1},{1,2},{2,3},{4,5},{5,6},{6,7},{8,9},{9,10},{10,11},{12,13},{... | collective-permute-start | bytes 12296 | tf_op jit(solution)/shard_map/ppermute | solution.py:20
  60.3 26.3 %collective-permute-start.12 = (f32[1,256,1024]{2,1,0:T(8,128)S(1)}, f32[1,256,1024]{2,1,0:T(8,128)S(1)}, u32[]{:S(2)}, u32[]{:S(2)}) collective-permute-start(f32[1,256,1024]{2,1,0:T(8,128)S(1)} %get-tuple-element.16), channel_id=1, source_target_pairs={{0,8},{4,12},{8,16},{12,20},{16,24},{20,28},{24,32},{28,36},{32,40... | collective-permute-start | bytes 3145736 | tf_op jit(solution)/shard_map/ppermute | solution.py:31
  64.5 6.8 %collective-permute-start.10 = (f32[1,1,1024]{2,1,0:T(1,128)S(1)}, f32[1,1,1024]{2,1,0:T(1,128)S(1)}, u32[]{:S(2)}, u32[]{:S(2)}) collective-permute-start(f32[1,1,1024]{2,1,0:T(1,128)S(1)} %get-tuple-element.47), channel_id=1, source_target_pairs={{1,0},{2,1},{3,2},{5,4},{6,5},{7,6},{9,8},{10,9},{11,10},{13,12},{... | collective-permute-start | bytes 12296 | tf_op jit(solution)/shard_map/ppermute | solution.py:23
  88.0 24.5 %collective-permute-start.13 = (f32[1,256,1024]{2,1,0:T(8,128)S(1)}, f32[1,256,1024]{2,1,0:T(8,128)S(1)}, u32[]{:S(2)}, u32[]{:S(2)}) collective-permute-start(f32[1,256,1024]{2,1,0:T(8,128)S(1)} %get-tuple-element.5), channel_id=1, source_target_pairs={{0,8},{4,12},{8,0},{12,4},{16,24},{20,28},{24,16},{28,20},{32,40},... | collective-permute-start | bytes 3145736 | tf_op jit(solution)/shard_map/ppermute | solution.py:37
  112.9 30.4 %collective-permute-start.16 = (f32[1,256,1024]{2,1,0:T(8,128)S(1)}, f32[1,256,1024]{2,1,0:T(8,128)S(1)}, u32[]{:S(2)}, u32[]{:S(2)}) collective-permute-start(f32[1,256,1024]{2,1,0:T(8,128)S(1)} %get-tuple-element.14), channel_id=1, source_target_pairs={{0,16},{4,20},{8,24},{12,28},{16,32},{20,36},{24,40},{28,44},{32,4... | collective-permute-start | bytes 3145736 | tf_op jit(solution)/shard_map/ppermute | solution.py:31
  122.7 6.8 %collective-permute-start.14 = (f32[1,1,1024]{2,1,0:T(1,128)S(1)}, f32[1,1,1024]{2,1,0:T(1,128)S(1)}, u32[]{:S(2)}, u32[]{:S(2)}) collective-permute-start(f32[1,1,1024]{2,1,0:T(1,128)S(1)} %get-tuple-element.45), channel_id=1, source_target_pairs={{1,0},{2,1},{3,2},{5,4},{6,5},{7,6},{9,8},{10,9},{11,10},{13,12},{... | collective-permute-start | bytes 12296 | tf_op jit(solution)/shard_map/ppermute | solution.py:23
  144.8 25.5 %collective-permute-start.17 = (f32[1,256,1024]{2,1,0:T(8,128)S(1)}, f32[1,256,1024]{2,1,0:T(8,128)S(1)}, u32[]{:S(2)}, u32[]{:S(2)}) collective-permute-start(f32[1,256,1024]{2,1,0:T(8,128)S(1)} %get-tuple-element.3), channel_id=1, source_target_pairs={{0,16},{4,20},{8,24},{12,28},{16,0},{20,4},{24,8},{28,12},{32,48},... | collective-permute-start | bytes 3145736 | tf_op jit(solution)/shard_map/ppermute | solution.py:37
  170.7 23.5 %collective-permute-start.20 = (f32[1,256,1024]{2,1,0:T(8,128)S(1)}, f32[1,256,1024]{2,1,0:T(8,128)S(1)}, u32[]{:S(2)}, u32[]{:S(2)}) collective-permute-start(f32[1,256,1024]{2,1,0:T(8,128)S(1)} %get-tuple-element.12), channel_id=1, source_target_pairs={{0,32},{4,36},{8,40},{12,44},{16,48},{20,52},{24,56},{28,60},{32,6... | collective-permute-start | bytes 3145736 | tf_op jit(solution)/shard_map/ppermute | solution.py:31
  176.1 6.8 %collective-permute-start.18 = (f32[1,1,1024]{2,1,0:T(1,128)S(1)}, f32[1,1,1024]{2,1,0:T(1,128)S(1)}, u32[]{:S(2)}, u32[]{:S(2)}) collective-permute-start(f32[1,1,1024]{2,1,0:T(1,128)S(1)} %get-tuple-element.43), channel_id=1, source_target_pairs={{1,0},{2,1},{3,2},{5,4},{6,5},{7,6},{9,8},{10,9},{11,10},{13,12},{... | collective-permute-start | bytes 12296 | tf_op jit(solution)/shard_map/ppermute | solution.py:23
  196.1 20.0 %collective-permute-start.23 = (f32[1,256,1024]{2,1,0:T(8,128)S(1)}, f32[1,256,1024]{2,1,0:T(8,128)S(1)}, u32[]{:S(2)}, u32[]{:S(2)}) collective-permute-start(f32[1,256,1024]{2,1,0:T(8,128)S(1)} %get-tuple-element.10), channel_id=1, source_target_pairs={{0,16},{4,20},{8,24},{12,28},{16,32},{20,36},{24,40},{28,44},{32,4... | collective-permute-start | bytes 3145736 | tf_op jit(solution)/shard_map/ppermute | solution.py:31
  198.6 6.8 %collective-permute-start.21 = (f32[1,1,1024]{2,1,0:T(1,128)S(1)}, f32[1,1,1024]{2,1,0:T(1,128)S(1)}, u32[]{:S(2)}, u32[]{:S(2)}) collective-permute-start(f32[1,1,1024]{2,1,0:T(1,128)S(1)} %get-tuple-element.41), channel_id=1, source_target_pairs={{1,0},{2,1},{3,2},{5,4},{6,5},{7,6},{9,8},{10,9},{11,10},{13,12},{... | collective-permute-start | bytes 12296 | tf_op jit(solution)/shard_map/ppermute | solution.py:23
  217.2 21.4 %collective-permute-start.26 = (f32[1,256,1024]{2,1,0:T(8,128)S(1)}, f32[1,256,1024]{2,1,0:T(8,128)S(1)}, u32[]{:S(2)}, u32[]{:S(2)}) collective-permute-start(f32[1,256,1024]{2,1,0:T(8,128)S(1)} %fusion.61), channel_id=1, source_target_pairs={{0,8},{4,12},{8,16},{12,20},{16,24},{20,28},{24,32},{28,36},{32,40... | collective-permute-start | bytes 3145736 | tf_op jit(solution)/shard_map/ppermute | solution.py:31
  221.4 6.8 %collective-permute-start.24 = (f32[1,1,1024]{2,1,0:T(1,128)S(1)}, f32[1,1,1024]{2,1,0:T(1,128)S(1)}, u32[]{:S(2)}, u32[]{:S(2)}) collective-permute-start(f32[1,1,1024]{2,1,0:T(1,128)S(1)} %get-tuple-element.39), channel_id=1, source_target_pairs={{1,0},{2,1},{3,2},{5,4},{6,5},{7,6},{9,8},{10,9},{11,10},{13,12},{... | collective-permute-start | bytes 12296 | tf_op jit(solution)/shard_map/ppermute | solution.py:23
  239.6 21.8 %collective-permute-start.29 = (f32[1,256,1024]{2,1,0:T(8,128)S(1)}, f32[1,256,1024]{2,1,0:T(8,128)S(1)}, u32[]{:S(2)}, u32[]{:S(2)}) collective-permute-start(f32[1,256,1024]{2,1,0:T(8,128)S(1)} %fusion.52), channel_id=1, source_target_pairs={{0,4},{4,8},{8,12},{12,16},{16,20},{20,24},{24,28},{28,32},{32,36}... | collective-permute-start | bytes 3145736 | tf_op jit(solution)/shard_map/ppermute | solution.py:31
  249.7 6.8 %collective-permute-start.27 = (f32[1,1,1024]{2,1,0:T(1,128)S(1)}, f32[1,1,1024]{2,1,0:T(1,128)S(1)}, u32[]{:S(2)}, u32[]{:S(2)}) collective-permute-start(f32[1,1,1024]{2,1,0:T(1,128)S(1)} %get-tuple-element.37), channel_id=1, source_target_pairs={{1,0},{2,1},{3,2},{5,4},{6,5},{7,6},{9,8},{10,9},{11,10},{13,12},{... | collective-permute-start | bytes 12296 | tf_op jit(solution)/shard_map/ppermute | solution.py:23
  264.2 31.5 %collective-permute-start.32 = (f32[1,256,1024]{2,1,0:T(8,128)}, f32[1,256,1024]{2,1,0:T(8,128)}, u32[]{:S(2)}, u32[]{:S(2)}) collective-permute-start(f32[1,256,1024]{2,1,0:T(8,128)} %get-tuple-element.22), channel_id=1, source_target_pairs={{0,4},{4,8},{8,12},{12,16},{16,20},{20,24},{24,28},{28,32},{32,36}... | collective-permute-start | bytes 3145736 | tf_op jit(solution)/shard_map/ppermute | solution.py:31
  269.8 18.6 %collective-permute-start.30 = (f32[2,1,1024]{2,1,0:T(1,128)S(1)}, f32[2,1,1024]{2,1,0:T(1,128)S(1)}, u32[]{:S(2)}, u32[]{:S(2)}) collective-permute-start(f32[2,1,1024]{2,1,0:T(1,128)S(1)} %get-tuple-element.25), channel_id=1, source_target_pairs={{1,0},{2,1},{3,2},{5,4},{6,5},{7,6},{9,8},{10,9},{11,10},{13,12},{... | collective-permute-start | bytes 24584 | tf_op jit(solution)/shard_map/ppermute | solution.py:23
  271.1 23.7 %collective-permute-start.31 = (f32[2,1,1024]{2,1,0:T(1,128)S(1)}, f32[2,1,1024]{2,1,0:T(1,128)S(1)}, u32[]{:S(2)}, u32[]{:S(2)}) collective-permute-start(f32[2,1,1024]{2,1,0:T(1,128)S(1)} %get-tuple-element.24), channel_id=1, source_target_pairs={{0,1},{1,2},{2,3},{4,5},{5,6},{6,7},{8,9},{9,10},{10,11},{12,13},{... | collective-permute-start | bytes 24584 | tf_op jit(solution)/shard_map/ppermute | solution.py:20
  277.5 36.1 %collective-permute-start.35 = (f32[1,256,1024]{2,1,0:T(8,128)}, f32[1,256,1024]{2,1,0:T(8,128)S(1)}, u32[]{:S(2)}, u32[]{:S(2)}) collective-permute-start(f32[1,256,1024]{2,1,0:T(8,128)} %get-tuple-element.11), channel_id=1, source_target_pairs={{0,32},{4,36},{8,40},{12,44},{16,48},{20,52},{24,56},{28,60},{32,6... | collective-permute-start | bytes 3145736 | tf_op jit(solution)/shard_map/ppermute | solution.py:31
  287.1 16.3 %collective-permute-start.33 = (f32[1,1,1024]{2,1,0:T(1,128)S(1)}, f32[1,1,1024]{2,1,0:T(1,128)S(1)}, u32[]{:S(2)}, u32[]{:S(2)}) collective-permute-start(f32[1,1,1024]{2,1,0:T(1,128)S(1)} %get-tuple-element.35), channel_id=1, source_target_pairs={{1,0},{2,1},{3,2},{5,4},{6,5},{7,6},{9,8},{10,9},{11,10},{13,12},{... | collective-permute-start | bytes 12296 | tf_op jit(solution)/shard_map/ppermute | solution.py:23
  288.5 15.0 %collective-permute-start.34 = (f32[1,1,1024]{2,1,0:T(1,128)S(1)}, f32[1,1,1024]{2,1,0:T(1,128)S(1)}, u32[]{:S(2)}, u32[]{:S(2)}) collective-permute-start(f32[1,1,1024]{2,1,0:T(1,128)S(1)} %get-tuple-element.34), channel_id=1, source_target_pairs={{0,1},{1,2},{2,3},{4,5},{5,6},{6,7},{8,9},{9,10},{10,11},{12,13},{... | collective-permute-start | bytes 12296 | tf_op jit(solution)/shard_map/ppermute | solution.py:20
  300.2 16.4 %collective-permute-start.38 = (f32[1,256,1024]{2,1,0:T(8,128)}, f32[1,256,1024]{2,1,0:T(8,128)}, u32[]{:S(2)}, u32[]{:S(2)}) collective-permute-start(f32[1,256,1024]{2,1,0:T(8,128)} %get-tuple-element.18), channel_id=1, source_target_pairs={{0,4},{4,8},{8,12},{12,16},{16,20},{20,24},{24,28},{28,32},{32,36}... | collective-permute-start | bytes 3145736 | tf_op jit(solution)/shard_map/ppermute | solution.py:31
  303.9 11.9 %collective-permute-start.36 = (f32[2,1,1024]{2,1,0:T(1,128)S(1)}, f32[2,1,1024]{2,1,0:T(1,128)S(1)}, u32[]{:S(2)}, u32[]{:S(2)}) collective-permute-start(f32[2,1,1024]{2,1,0:T(1,128)S(1)} %get-tuple-element.21), channel_id=1, source_target_pairs={{1,0},{2,1},{3,2},{5,4},{6,5},{7,6},{9,8},{10,9},{11,10},{13,12},{... | collective-permute-start | bytes 24584 | tf_op jit(solution)/shard_map/ppermute | solution.py:23
  305.2 10.6 %collective-permute-start.37 = (f32[2,1,1024]{2,1,0:T(1,128)S(1)}, f32[2,1,1024]{2,1,0:T(1,128)S(1)}, u32[]{:S(2)}, u32[]{:S(2)}) collective-permute-start(f32[2,1,1024]{2,1,0:T(1,128)S(1)} %get-tuple-element.20), channel_id=1, source_target_pairs={{0,1},{1,2},{2,3},{4,5},{5,6},{6,7},{8,9},{9,10},{10,11},{12,13},{... | collective-permute-start | bytes 24584 | tf_op jit(solution)/shard_map/ppermute | solution.py:20
  (22 other events, 174.4 us)
where the time goes:
time: 393 us; the launch traced here: 391 us
  starting transfers between devices  157 us (40%)
  waiting for transfers between devices  124 us (32%)
  blocking collectives  66.9 us (17%)
  other arithmetic  30.2 us (8%)
  local copies, waits for them, and re-layouts  9.37 us (2%)
    ppermute x12, waiting for transfers between devices, shifted(): lax.ppermute(value, axis, [(source, source + steps) for source in range(f...  70.9 us
    ppermute x12, starting transfers between devices, with_halo(): lax.ppermute(lax.slice_in_dim(block, block.shape[dim] - width, None, axis...  68.3 us
    psum x5, blocking collectives, over_axes(): array = lax.psum(array, axis)  66.9 us
    ppermute x12, starting transfers between devices, shifted(): lax.ppermute(value, axis, [(source, source + steps) for source in range(f...  66.8 us
    ppermute x3, waiting for transfers between devices, from_partner(): return lax.ppermute(value, axis, pairs)  46.1 us
    ppermute x12, starting transfers between devices, with_halo(): lax.ppermute(lax.slice_in_dim(block, 0, width, axis=dim), axis, backward)  15.5 us
    reduce_sum x6, other arithmetic, record(): local_part = jnp.sum(resid * resid) * weight_of(level)  11.7 us
  transfers between devices with their start and end apart: 39, of which 22 were waited for; matrix products, arithmetic and copies ran while one was open for 3% of the time, Pallas kernels for 0%

commit v1 on v0

--- a/solution.py
+++ b/solution.py
@@ -38,9 +38,7 @@
 
 
 def over_axes(array, axes):
-    for axis in axes:
-        array = lax.psum(array, axis)
-    return array
+    return lax.psum(array, axes)
 
 
 def neighbours(field):

time: 393 us -> 433 us (1.10)
  blocking collectives: 66.9 us -> 108 us
    psum x5 -> x1, blocking collectives: 66.9 us -> 108 us  [over_axes(): return lax.psum(array, axes)]
where the time goes in v1:
time: 433 us; the launch traced here: 432 us
  starting transfers between devices  157 us (36%)
  waiting for transfers between devices  124 us (29%)
  blocking collectives  108 us (25%)
  other arithmetic  30.2 us (7%)
  local copies, waits for them, and re-layouts  9.38 us (2%)
    psum x1, blocking collectives, over_axes(): return lax.psum(array, axes)  108 us
    ppermute x12, waiting for transfers between devices, shifted(): lax.ppermute(value, axis, [(source, source + steps) for source in range(f...  70.9 us
    ppermute x12, starting transfers between devices, with_halo(): lax.ppermute(lax.slice_in_dim(block, block.shape[dim] - width, None, axis...  68.3 us
    ppermute x12, starting transfers between devices, shifted(): lax.ppermute(value, axis, [(source, source + steps) for source in range(f...  66.8 us
    ppermute x3, waiting for transfers between devices, from_partner(): return lax.ppermute(value, axis, pairs)  46.2 us
    ppermute x12, starting transfers between devices, with_halo(): lax.ppermute(lax.slice_in_dim(block, 0, width, axis=dim), axis, backward)  15.5 us
    reduce_sum x6, other arithmetic, record(): local_part = jnp.sum(resid * resid) * weight_of(level)  11.6 us
  transfers between devices with their start and end apart: 39, of which 22 were waited for; matrix products, arithmetic and copies ran while one was open for 3% of the time, Pallas kernels for 0%

profile of v1, /device:TPU:1, one launch (start us, length us, event | category | flops | bytes accessed | tf_op | source)
XLA Modules:
  0.0 431.9 jit_solution(11757372127027365394)
XLA Ops:
  2.5 4.5 %collective-permute-start.2 = (f32[1,256,1024]{2,1,0:T(8,128)S(1)}, f32[1,256,1024]{2,1,0:T(8,128)S(1)}, u32[]{:S(2)}, u32[]{:S(2)}) collective-permute-start(f32[1,256,1024]{2,1,0:T(8,128)S(1)} %get-tuple-element.30), channel_id=1, source_target_pairs={{0,4},{4,8},{8,12},{12,16},{16,20},{20,24},{24,28},{28,32},{32,36}... | collective-permute-start | bytes 3145736 | tf_op jit(solution)/shard_map/ppermute | solution.py:31
  8.4 5.5 %collective-permute-start.1 = (f32[2,1,1024]{2,1,0:T(1,128)S(1)}, f32[2,1,1024]{2,1,0:T(1,128)S(1)}, u32[]{:S(2)}, u32[]{:S(2)}) collective-permute-start(f32[2,1,1024]{2,1,0:T(1,128)S(1)} %get-tuple-element.32), channel_id=1, source_target_pairs={{0,1},{1,2},{2,3},{4,5},{5,6},{6,7},{8,9},{9,10},{10,11},{12,13},{... | collective-permute-start | bytes 24584 | tf_op jit(solution)/shard_map/ppermute | solution.py:20
  20.8 4.4 %collective-permute-start.5 = (f32[1,256,1024]{2,1,0:T(8,128)S(1)}, f32[1,256,1024]{2,1,0:T(8,128)S(1)}, u32[]{:S(2)}, u32[]{:S(2)}) collective-permute-start(f32[1,256,1024]{2,1,0:T(8,128)S(1)} %get-tuple-element.28), channel_id=1, source_target_pairs={{0,4},{4,8},{8,12},{12,16},{16,20},{20,24},{24,28},{28,32},{32,36}... | collective-permute-start | bytes 3145736 | tf_op jit(solution)/shard_map/ppermute | solution.py:31
  26.5 5.5 %collective-permute-start.4 = (f32[2,1,1024]{2,1,0:T(1,128)S(1)}, f32[2,1,1024]{2,1,0:T(1,128)S(1)}, u32[]{:S(2)}, u32[]{:S(2)}) collective-permute-start(f32[2,1,1024]{2,1,0:T(1,128)S(1)} %get-tuple-element.26), channel_id=1, source_target_pairs={{0,1},{1,2},{2,3},{4,5},{5,6},{6,7},{8,9},{9,10},{10,11},{12,13},{... | collective-permute-start | bytes 24584 | tf_op jit(solution)/shard_map/ppermute | solution.py:20
  39.6 4.4 %collective-permute-start.8 = (f32[1,256,1024]{2,1,0:T(8,128)S(1)}, f32[1,256,1024]{2,1,0:T(8,128)S(1)}, u32[]{:S(2)}, u32[]{:S(2)}) collective-permute-start(f32[1,256,1024]{2,1,0:T(8,128)S(1)} %bitcast_divide_fusion.3), channel_id=1, source_target_pairs={{0,4},{4,8},{8,12},{12,16},{16,20},{20,24},{24,28},{28,32},{32,36}... | collective-permute-start | bytes 3145736 | tf_op jit(solution)/shard_map/ppermute | solution.py:31
  45.3 5.5 %collective-permute-start.7 = (f32[1,1,1024]{2,1,0:T(1,128)S(1)}, f32[1,1,1024]{2,1,0:T(1,128)S(1)}, u32[]{:S(2)}, u32[]{:S(2)}) collective-permute-start(f32[1,1,1024]{2,1,0:T(1,128)S(1)} %get-tuple-element.48), channel_id=1, source_target_pairs={{0,1},{1,2},{2,3},{4,5},{5,6},{6,7},{8,9},{9,10},{10,11},{12,13},{... | collective-permute-start | bytes 12296 | tf_op jit(solution)/shard_map/ppermute | solution.py:20
  60.3 4.2 collective-permute-start.12
  65.8 5.5 %collective-permute-start.11 = (f32[1,1,1024]{2,1,0:T(1,128)S(1)}, f32[1,1,1024]{2,1,0:T(1,128)S(1)}, u32[]{:S(2)}, u32[]{:S(2)}) collective-permute-start(f32[1,1,1024]{2,1,0:T(1,128)S(1)} %get-tuple-element.46), channel_id=1, source_target_pairs={{0,1},{1,2},{2,3},{4,5},{5,6},{6,7},{8,9},{9,10},{10,11},{12,13},{... | collective-permute-start | bytes 12296 | tf_op jit(solution)/shard_map/ppermute | solution.py:20
  72.5 14.1 %collective-permute-done.12 = f32[1,256,1024]{2,1,0:T(8,128)S(1)} collective-permute-done((f32[1,256,1024]{2,1,0:T(8,128)S(1)}, f32[1,256,1024]{2,1,0:T(8,128)S(1)}, u32[]{:S(2)}, u32[]{:S(2)}) %collective-permute-start.12) | collective-permute-done | bytes 1048608 | tf_op jit(solution)/shard_map/ppermute | solution.py:31
  90.2 22.3 %collective-permute-done.13 = f32[1,256,1024]{2,1,0:T(8,128)S(1)} collective-permute-done((f32[1,256,1024]{2,1,0:T(8,128)S(1)}, f32[1,256,1024]{2,1,0:T(8,128)S(1)}, u32[]{:S(2)}, u32[]{:S(2)}) %collective-permute-start.13) | collective-permute-done | bytes 1048608 | tf_op jit(solution)/shard_map/ppermute | solution.py:37
  112.9 9.8 %collective-permute-start.16 = (f32[1,256,1024]{2,1,0:T(8,128)S(1)}, f32[1,256,1024]{2,1,0:T(8,128)S(1)}, u32[]{:S(2)}, u32[]{:S(2)}) collective-permute-start(f32[1,256,1024]{2,1,0:T(8,128)S(1)} %get-tuple-element.14), channel_id=1, source_target_pairs={{0,16},{4,20},{8,24},{12,28},{16,32},{20,36},{24,40},{28,44},{32,4... | collective-permute-start | bytes 3145736 | tf_op jit(solution)/shard_map/ppermute | solution.py:31
  124.0 5.5 %collective-permute-start.15 = (f32[1,1,1024]{2,1,0:T(1,128)S(1)}, f32[1,1,1024]{2,1,0:T(1,128)S(1)}, u32[]{:S(2)}, u32[]{:S(2)}) collective-permute-start(f32[1,1,1024]{2,1,0:T(1,128)S(1)} %get-tuple-element.44), channel_id=1, source_target_pairs={{0,1},{1,2},{2,3},{4,5},{5,6},{6,7},{8,9},{9,10},{10,11},{12,13},{... | collective-permute-start | bytes 12296 | tf_op jit(solution)/shard_map/ppermute | solution.py:20
  130.7 12.6 %collective-permute-done.16 = f32[1,256,1024]{2,1,0:T(8,128)S(1)} collective-permute-done((f32[1,256,1024]{2,1,0:T(8,128)S(1)}, f32[1,256,1024]{2,1,0:T(8,128)S(1)}, u32[]{:S(2)}, u32[]{:S(2)}) %collective-permute-start.16) | collective-permute-done | bytes 1048608 | tf_op jit(solution)/shard_map/ppermute | solution.py:31
  144.7 4.3 %collective-permute-start.17 = (f32[1,256,1024]{2,1,0:T(8,128)S(1)}, f32[1,256,1024]{2,1,0:T(8,128)S(1)}, u32[]{:S(2)}, u32[]{:S(2)}) collective-permute-start(f32[1,256,1024]{2,1,0:T(8,128)S(1)} %get-tuple-element.3), channel_id=1, source_target_pairs={{0,16},{4,20},{8,24},{12,28},{16,0},{20,4},{24,8},{28,12},{32,48},... | collective-permute-start | bytes 3145736 | tf_op jit(solution)/shard_map/ppermute | solution.py:37
  149.1 21.2 %collective-permute-done.17 = f32[1,256,1024]{2,1,0:T(8,128)S(1)} collective-permute-done((f32[1,256,1024]{2,1,0:T(8,128)S(1)}, f32[1,256,1024]{2,1,0:T(8,128)S(1)}, u32[]{:S(2)}, u32[]{:S(2)}) %collective-permute-start.17) | collective-permute-done | bytes 1048608 | tf_op jit(solution)/shard_map/ppermute | solution.py:37
  170.7 5.3 %collective-permute-start.20 = (f32[1,256,1024]{2,1,0:T(8,128)S(1)}, f32[1,256,1024]{2,1,0:T(8,128)S(1)}, u32[]{:S(2)}, u32[]{:S(2)}) collective-permute-start(f32[1,256,1024]{2,1,0:T(8,128)S(1)} %get-tuple-element.12), channel_id=1, source_target_pairs={{0,32},{4,36},{8,40},{12,44},{16,48},{20,52},{24,56},{28,60},{32,6... | collective-permute-start | bytes 3145736 | tf_op jit(solution)/shard_map/ppermute | solution.py:31
  177.3 5.5 %collective-permute-start.19 = (f32[1,1,1024]{2,1,0:T(1,128)S(1)}, f32[1,1,1024]{2,1,0:T(1,128)S(1)}, u32[]{:S(2)}, u32[]{:S(2)}) collective-permute-start(f32[1,1,1024]{2,1,0:T(1,128)S(1)} %get-tuple-element.42), channel_id=1, source_target_pairs={{0,1},{1,2},{2,3},{4,5},{5,6},{6,7},{8,9},{9,10},{10,11},{12,13},{... | collective-permute-start | bytes 12296 | tf_op jit(solution)/shard_map/ppermute | solution.py:20
  184.0 10.0 %collective-permute-done.20 = f32[1,256,1024]{2,1,0:T(8,128)S(1)} collective-permute-done((f32[1,256,1024]{2,1,0:T(8,128)S(1)}, f32[1,256,1024]{2,1,0:T(8,128)S(1)}, u32[]{:S(2)}, u32[]{:S(2)}) %collective-permute-start.20) | collective-permute-done | bytes 1048608 | tf_op jit(solution)/shard_map/ppermute | solution.py:31
  199.8 5.5 %collective-permute-start.22 = (f32[1,1,1024]{2,1,0:T(1,128)S(1)}, f32[1,1,1024]{2,1,0:T(1,128)S(1)}, u32[]{:S(2)}, u32[]{:S(2)}) collective-permute-start(f32[1,1,1024]{2,1,0:T(1,128)S(1)} %get-tuple-element.40), channel_id=1, source_target_pairs={{0,1},{1,2},{2,3},{4,5},{5,6},{6,7},{8,9},{9,10},{10,11},{12,13},{... | collective-permute-start | bytes 12296 | tf_op jit(solution)/shard_map/ppermute | solution.py:20
  206.5 9.4 %collective-permute-done.23 = f32[1,256,1024]{2,1,0:T(8,128)S(1)} collective-permute-done((f32[1,256,1024]{2,1,0:T(8,128)S(1)}, f32[1,256,1024]{2,1,0:T(8,128)S(1)}, u32[]{:S(2)}, u32[]{:S(2)}) %collective-permute-start.23) | collective-permute-done | bytes 1048608 | tf_op jit(solution)/shard_map/ppermute | solution.py:31
  217.1 4.2 collective-permute-start.26
  222.6 5.5 %collective-permute-start.25 = (f32[1,1,1024]{2,1,0:T(1,128)S(1)}, f32[1,1,1024]{2,1,0:T(1,128)S(1)}, u32[]{:S(2)}, u32[]{:S(2)}) collective-permute-start(f32[1,1,1024]{2,1,0:T(1,128)S(1)} %get-tuple-element.38), channel_id=1, source_target_pairs={{0,1},{1,2},{2,3},{4,5},{5,6},{6,7},{8,9},{9,10},{10,11},{12,13},{... | collective-permute-start | bytes 12296 | tf_op jit(solution)/shard_map/ppermute | solution.py:20
  229.3 9.1 %collective-permute-done.26 = f32[1,256,1024]{2,1,0:T(8,128)S(1)} collective-permute-done((f32[1,256,1024]{2,1,0:T(8,128)S(1)}, f32[1,256,1024]{2,1,0:T(8,128)S(1)}, u32[]{:S(2)}, u32[]{:S(2)}) %collective-permute-start.26) | collective-permute-done | bytes 1048608 | tf_op jit(solution)/shard_map/ppermute | solution.py:31
  239.4 10.1 %collective-permute-start.29 = (f32[1,256,1024]{2,1,0:T(8,128)S(1)}, f32[1,256,1024]{2,1,0:T(8,128)S(1)}, u32[]{:S(2)}, u32[]{:S(2)}) collective-permute-start(f32[1,256,1024]{2,1,0:T(8,128)S(1)} %fusion.52), channel_id=1, source_target_pairs={{0,4},{4,8},{8,12},{12,16},{16,20},{20,24},{24,28},{28,32},{32,36}... | collective-permute-start | bytes 3145736 | tf_op jit(solution)/shard_map/ppermute | solution.py:31
  250.9 5.5 %collective-permute-start.28 = (f32[1,1,1024]{2,1,0:T(1,128)S(1)}, f32[1,1,1024]{2,1,0:T(1,128)S(1)}, u32[]{:S(2)}, u32[]{:S(2)}) collective-permute-start(f32[1,1,1024]{2,1,0:T(1,128)S(1)} %get-tuple-element.36), channel_id=1, source_target_pairs={{0,1},{1,2},{2,3},{4,5},{5,6},{6,7},{8,9},{9,10},{10,11},{12,13},{... | collective-permute-start | bytes 12296 | tf_op jit(solution)/shard_map/ppermute | solution.py:20
  257.6 3.7 collective-permute-done.29
  264.0 4.4 %collective-permute-start.32 = (f32[1,256,1024]{2,1,0:T(8,128)}, f32[1,256,1024]{2,1,0:T(8,128)}, u32[]{:S(2)}, u32[]{:S(2)}) collective-permute-start(f32[1,256,1024]{2,1,0:T(8,128)} %get-tuple-element.22), channel_id=1, source_target_pairs={{0,4},{4,8},{8,12},{12,16},{16,20},{20,24},{24,28},{28,32},{32,36}... | collective-permute-start | bytes 3145736 | tf_op jit(solution)/shard_map/ppermute | solution.py:31
  271.0 5.5 %collective-permute-start.31 = (f32[2,1,1024]{2,1,0:T(1,128)S(1)}, f32[2,1,1024]{2,1,0:T(1,128)S(1)}, u32[]{:S(2)}, u32[]{:S(2)}) collective-permute-start(f32[2,1,1024]{2,1,0:T(1,128)S(1)} %get-tuple-element.24), channel_id=1, source_target_pairs={{0,1},{1,2},{2,3},{4,5},{5,6},{6,7},{8,9},{9,10},{10,11},{12,13},{... | collective-permute-start | bytes 24584 | tf_op jit(solution)/shard_map/ppermute | solution.py:20
  277.3 9.8 %collective-permute-start.35 = (f32[1,256,1024]{2,1,0:T(8,128)}, f32[1,256,1024]{2,1,0:T(8,128)S(1)}, u32[]{:S(2)}, u32[]{:S(2)}) collective-permute-start(f32[1,256,1024]{2,1,0:T(8,128)} %get-tuple-element.11), channel_id=1, source_target_pairs={{0,32},{4,36},{8,40},{12,44},{16,48},{20,52},{24,56},{28,60},{32,6... | collective-permute-start | bytes 3145736 | tf_op jit(solution)/shard_map/ppermute | solution.py:31
  288.4 6.4 %collective-permute-start.34 = (f32[1,1,1024]{2,1,0:T(1,128)S(1)}, f32[1,1,1024]{2,1,0:T(1,128)S(1)}, u32[]{:S(2)}, u32[]{:S(2)}) collective-permute-start(f32[1,1,1024]{2,1,0:T(1,128)S(1)} %get-tuple-element.34), channel_id=1, source_target_pairs={{0,1},{1,2},{2,3},{4,5},{5,6},{6,7},{8,9},{9,10},{10,11},{12,13},{... | collective-permute-start | bytes 12296 | tf_op jit(solution)/shard_map/ppermute | solution.py:20
  305.2 6.7 %collective-permute-start.37 = (f32[2,1,1024]{2,1,0:T(1,128)S(1)}, f32[2,1,1024]{2,1,0:T(1,128)S(1)}, u32[]{:S(2)}, u32[]{:S(2)}) collective-permute-start(f32[2,1,1024]{2,1,0:T(1,128)S(1)} %get-tuple-element.20), channel_id=1, source_target_pairs={{0,1},{1,2},{2,3},{4,5},{5,6},{6,7},{8,9},{9,10},{10,11},{12,13},{... | collective-permute-start | bytes 24584 | tf_op jit(solution)/shard_map/ppermute | solution.py:20
  323.2 108.2 %psum.7 = f32[6]{0:T(128)S(1)} all-reduce(f32[6]{0:T(128)S(1)} %stack.27), channel_id=1, replica_groups=mesh['tm_0'=2,'tm_1'=4,'tm_2'=4,'tm_3'=2,'space'=4] {'tm_0','tm_1','tm_2..., use_global_device_ids=true, to_apply=%region_6.7 | all-reduce | flops 6 | bytes 48 | tf_op jit(solution)/shard_map/psum | solution.py:41
  (125 shorter events, 84.1 us)
Async XLA Ops:
  2.5 16.2 %collective-permute-start.2 = (f32[1,256,1024]{2,1,0:T(8,128)S(1)}, f32[1,256,1024]{2,1,0:T(8,128)S(1)}, u32[]{:S(2)}, u32[]{:S(2)}) collective-permute-start(f32[1,256,1024]{2,1,0:T(8,128)S(1)} %get-tuple-element.30), channel_id=1, source_target_pairs={{0,4},{4,8},{8,12},{12,16},{16,20},{20,24},{24,28},{28,32},{32,36}... | collective-permute-start | bytes 3145736 | tf_op jit(solution)/shard_map/ppermute | solution.py:31
  7.1 7.0 %collective-permute-start = (f32[2,1,1024]{2,1,0:T(1,128)S(1)}, f32[2,1,1024]{2,1,0:T(1,128)S(1)}, u32[]{:S(2)}, u32[]{:S(2)}) collective-permute-start(f32[2,1,1024]{2,1,0:T(1,128)S(1)} %get-tuple-element.33), channel_id=1, source_target_pairs={{1,0},{2,1},{3,2},{5,4},{6,5},{7,6},{9,8},{10,9},{11,10},{13,12},{... | collective-permute-start | bytes 24584 | tf_op jit(solution)/shard_map/ppermute | solution.py:23
  8.4 6.3 %collective-permute-start.1 = (f32[2,1,1024]{2,1,0:T(1,128)S(1)}, f32[2,1,1024]{2,1,0:T(1,128)S(1)}, u32[]{:S(2)}, u32[]{:S(2)}) collective-permute-start(f32[2,1,1024]{2,1,0:T(1,128)S(1)} %get-tuple-element.32), channel_id=1, source_target_pairs={{0,1},{1,2},{2,3},{4,5},{5,6},{6,7},{8,9},{9,10},{10,11},{12,13},{... | collective-permute-start | bytes 24584 | tf_op jit(solution)/shard_map/ppermute | solution.py:20
  20.8 16.1 %collective-permute-start.5 = (f32[1,256,1024]{2,1,0:T(8,128)S(1)}, f32[1,256,1024]{2,1,0:T(8,128)S(1)}, u32[]{:S(2)}, u32[]{:S(2)}) collective-permute-start(f32[1,256,1024]{2,1,0:T(8,128)S(1)} %get-tuple-element.28), channel_id=1, source_target_pairs={{0,4},{4,8},{8,12},{12,16},{16,20},{20,24},{24,28},{28,32},{32,36}... | collective-permute-start | bytes 3145736 | tf_op jit(solution)/shard_map/ppermute | solution.py:31
  25.2 6.8 %collective-permute-start.3 = (f32[2,1,1024]{2,1,0:T(1,128)S(1)}, f32[2,1,1024]{2,1,0:T(1,128)S(1)}, u32[]{:S(2)}, u32[]{:S(2)}) collective-permute-start(f32[2,1,1024]{2,1,0:T(1,128)S(1)} %get-tuple-element.27), channel_id=1, source_target_pairs={{1,0},{2,1},{3,2},{5,4},{6,5},{7,6},{9,8},{10,9},{11,10},{13,12},{... | collective-permute-start | bytes 24584 | tf_op jit(solution)/shard_map/ppermute | solution.py:23
  26.5 6.3 %collective-permute-start.4 = (f32[2,1,1024]{2,1,0:T(1,128)S(1)}, f32[2,1,1024]{2,1,0:T(1,128)S(1)}, u32[]{:S(2)}, u32[]{:S(2)}) collective-permute-start(f32[2,1,1024]{2,1,0:T(1,128)S(1)} %get-tuple-element.26), channel_id=1, source_target_pairs={{0,1},{1,2},{2,3},{4,5},{5,6},{6,7},{8,9},{9,10},{10,11},{12,13},{... | collective-permute-start | bytes 24584 | tf_op jit(solution)/shard_map/ppermute | solution.py:20
  39.6 16.1 %collective-permute-start.8 = (f32[1,256,1024]{2,1,0:T(8,128)S(1)}, f32[1,256,1024]{2,1,0:T(8,128)S(1)}, u32[]{:S(2)}, u32[]{:S(2)}) collective-permute-start(f32[1,256,1024]{2,1,0:T(8,128)S(1)} %bitcast_divide_fusion.3), channel_id=1, source_target_pairs={{0,4},{4,8},{8,12},{12,16},{16,20},{20,24},{24,28},{28,32},{32,36}... | collective-permute-start | bytes 3145736 | tf_op jit(solution)/shard_map/ppermute | solution.py:31
  44.0 6.8 %collective-permute-start.6 = (f32[1,1,1024]{2,1,0:T(1,128)S(1)}, f32[1,1,1024]{2,1,0:T(1,128)S(1)}, u32[]{:S(2)}, u32[]{:S(2)}) collective-permute-start(f32[1,1,1024]{2,1,0:T(1,128)S(1)} %get-tuple-element.49), channel_id=1, source_target_pairs={{1,0},{2,1},{3,2},{5,4},{6,5},{7,6},{9,8},{10,9},{11,10},{13,12},{... | collective-permute-start | bytes 12296 | tf_op jit(solution)/shard_map/ppermute | solution.py:23
  60.3 26.3 %collective-permute-start.12 = (f32[1,256,1024]{2,1,0:T(8,128)S(1)}, f32[1,256,1024]{2,1,0:T(8,128)S(1)}, u32[]{:S(2)}, u32[]{:S(2)}) collective-permute-start(f32[1,256,1024]{2,1,0:T(8,128)S(1)} %get-tuple-element.16), channel_id=1, source_target_pairs={{0,8},{4,12},{8,16},{12,20},{16,24},{20,28},{24,32},{28,36},{32,40... | collective-permute-start | bytes 3145736 | tf_op jit(solution)/shard_map/ppermute | solution.py:31
  64.5 6.8 %collective-permute-start.10 = (f32[1,1,1024]{2,1,0:T(1,128)S(1)}, f32[1,1,1024]{2,1,0:T(1,128)S(1)}, u32[]{:S(2)}, u32[]{:S(2)}) collective-permute-start(f32[1,1,1024]{2,1,0:T(1,128)S(1)} %get-tuple-element.47), channel_id=1, source_target_pairs={{1,0},{2,1},{3,2},{5,4},{6,5},{7,6},{9,8},{10,9},{11,10},{13,12},{... | collective-permute-start | bytes 12296 | tf_op jit(solution)/shard_map/ppermute | solution.py:23
  88.0 24.5 %collective-permute-start.13 = (f32[1,256,1024]{2,1,0:T(8,128)S(1)}, f32[1,256,1024]{2,1,0:T(8,128)S(1)}, u32[]{:S(2)}, u32[]{:S(2)}) collective-permute-start(f32[1,256,1024]{2,1,0:T(8,128)S(1)} %get-tuple-element.5), channel_id=1, source_target_pairs={{0,8},{4,12},{8,0},{12,4},{16,24},{20,28},{24,16},{28,20},{32,40},... | collective-permute-start | bytes 3145736 | tf_op jit(solution)/shard_map/ppermute | solution.py:37
  112.9 30.4 %collective-permute-start.16 = (f32[1,256,1024]{2,1,0:T(8,128)S(1)}, f32[1,256,1024]{2,1,0:T(8,128)S(1)}, u32[]{:S(2)}, u32[]{:S(2)}) collective-permute-start(f32[1,256,1024]{2,1,0:T(8,128)S(1)} %get-tuple-element.14), channel_id=1, source_target_pairs={{0,16},{4,20},{8,24},{12,28},{16,32},{20,36},{24,40},{28,44},{32,4... | collective-permute-start | bytes 3145736 | tf_op jit(solution)/shard_map/ppermute | solution.py:31
  122.7 6.8 %collective-permute-start.14 = (f32[1,1,1024]{2,1,0:T(1,128)S(1)}, f32[1,1,1024]{2,1,0:T(1,128)S(1)}, u32[]{:S(2)}, u32[]{:S(2)}) collective-permute-start(f32[1,1,1024]{2,1,0:T(1,128)S(1)} %get-tuple-element.45), channel_id=1, source_target_pairs={{1,0},{2,1},{3,2},{5,4},{6,5},{7,6},{9,8},{10,9},{11,10},{13,12},{... | collective-permute-start | bytes 12296 | tf_op jit(solution)/shard_map/ppermute | solution.py:23
  124.0 6.3 %collective-permute-start.15 = (f32[1,1,1024]{2,1,0:T(1,128)S(1)}, f32[1,1,1024]{2,1,0:T(1,128)S(1)}, u32[]{:S(2)}, u32[]{:S(2)}) collective-permute-start(f32[1,1,1024]{2,1,0:T(1,128)S(1)} %get-tuple-element.44), channel_id=1, source_target_pairs={{0,1},{1,2},{2,3},{4,5},{5,6},{6,7},{8,9},{9,10},{10,11},{12,13},{... | collective-permute-start | bytes 12296 | tf_op jit(solution)/shard_map/ppermute | solution.py:20
  144.7 25.5 %collective-permute-start.17 = (f32[1,256,1024]{2,1,0:T(8,128)S(1)}, f32[1,256,1024]{2,1,0:T(8,128)S(1)}, u32[]{:S(2)}, u32[]{:S(2)}) collective-permute-start(f32[1,256,1024]{2,1,0:T(8,128)S(1)} %get-tuple-element.3), channel_id=1, source_target_pairs={{0,16},{4,20},{8,24},{12,28},{16,0},{20,4},{24,8},{28,12},{32,48},... | collective-permute-start | bytes 3145736 | tf_op jit(solution)/shard_map/ppermute | solution.py:37
  170.7 23.3 %collective-permute-start.20 = (f32[1,256,1024]{2,1,0:T(8,128)S(1)}, f32[1,256,1024]{2,1,0:T(8,128)S(1)}, u32[]{:S(2)}, u32[]{:S(2)}) collective-permute-start(f32[1,256,1024]{2,1,0:T(8,128)S(1)} %get-tuple-element.12), channel_id=1, source_target_pairs={{0,32},{4,36},{8,40},{12,44},{16,48},{20,52},{24,56},{28,60},{32,6... | collective-permute-start | bytes 3145736 | tf_op jit(solution)/shard_map/ppermute | solution.py:31
  176.0 6.8 %collective-permute-start.18 = (f32[1,1,1024]{2,1,0:T(1,128)S(1)}, f32[1,1,1024]{2,1,0:T(1,128)S(1)}, u32[]{:S(2)}, u32[]{:S(2)}) collective-permute-start(f32[1,1,1024]{2,1,0:T(1,128)S(1)} %get-tuple-element.43), channel_id=1, source_target_pairs={{1,0},{2,1},{3,2},{5,4},{6,5},{7,6},{9,8},{10,9},{11,10},{13,12},{... | collective-permute-start | bytes 12296 | tf_op jit(solution)/shard_map/ppermute | solution.py:23
  196.0 20.0 %collective-permute-start.23 = (f32[1,256,1024]{2,1,0:T(8,128)S(1)}, f32[1,256,1024]{2,1,0:T(8,128)S(1)}, u32[]{:S(2)}, u32[]{:S(2)}) collective-permute-start(f32[1,256,1024]{2,1,0:T(8,128)S(1)} %get-tuple-element.10), channel_id=1, source_target_pairs={{0,16},{4,20},{8,24},{12,28},{16,32},{20,36},{24,40},{28,44},{32,4... | collective-permute-start | bytes 3145736 | tf_op jit(solution)/shard_map/ppermute | solution.py:31
  198.5 6.8 %collective-permute-start.21 = (f32[1,1,1024]{2,1,0:T(1,128)S(1)}, f32[1,1,1024]{2,1,0:T(1,128)S(1)}, u32[]{:S(2)}, u32[]{:S(2)}) collective-permute-start(f32[1,1,1024]{2,1,0:T(1,128)S(1)} %get-tuple-element.41), channel_id=1, source_target_pairs={{1,0},{2,1},{3,2},{5,4},{6,5},{7,6},{9,8},{10,9},{11,10},{13,12},{... | collective-permute-start | bytes 12296 | tf_op jit(solution)/shard_map/ppermute | solution.py:23
  217.1 21.4 %collective-permute-start.26 = (f32[1,256,1024]{2,1,0:T(8,128)S(1)}, f32[1,256,1024]{2,1,0:T(8,128)S(1)}, u32[]{:S(2)}, u32[]{:S(2)}) collective-permute-start(f32[1,256,1024]{2,1,0:T(8,128)S(1)} %fusion.61), channel_id=1, source_target_pairs={{0,8},{4,12},{8,16},{12,20},{16,24},{20,28},{24,32},{28,36},{32,40... | collective-permute-start | bytes 3145736 | tf_op jit(solution)/shard_map/ppermute | solution.py:31
  221.3 6.8 %collective-permute-start.24 = (f32[1,1,1024]{2,1,0:T(1,128)S(1)}, f32[1,1,1024]{2,1,0:T(1,128)S(1)}, u32[]{:S(2)}, u32[]{:S(2)}) collective-permute-start(f32[1,1,1024]{2,1,0:T(1,128)S(1)} %get-tuple-element.39), channel_id=1, source_target_pairs={{1,0},{2,1},{3,2},{5,4},{6,5},{7,6},{9,8},{10,9},{11,10},{13,12},{... | collective-permute-start | bytes 12296 | tf_op jit(solution)/shard_map/ppermute | solution.py:23
  239.4 21.9 %collective-permute-start.29 = (f32[1,256,1024]{2,1,0:T(8,128)S(1)}, f32[1,256,1024]{2,1,0:T(8,128)S(1)}, u32[]{:S(2)}, u32[]{:S(2)}) collective-permute-start(f32[1,256,1024]{2,1,0:T(8,128)S(1)} %fusion.52), channel_id=1, source_target_pairs={{0,4},{4,8},{8,12},{12,16},{16,20},{20,24},{24,28},{28,32},{32,36}... | collective-permute-start | bytes 3145736 | tf_op jit(solution)/shard_map/ppermute | solution.py:31
  249.6 6.8 %collective-permute-start.27 = (f32[1,1,1024]{2,1,0:T(1,128)S(1)}, f32[1,1,1024]{2,1,0:T(1,128)S(1)}, u32[]{:S(2)}, u32[]{:S(2)}) collective-permute-start(f32[1,1,1024]{2,1,0:T(1,128)S(1)} %get-tuple-element.37), channel_id=1, source_target_pairs={{1,0},{2,1},{3,2},{5,4},{6,5},{7,6},{9,8},{10,9},{11,10},{13,12},{... | collective-permute-start | bytes 12296 | tf_op jit(solution)/shard_map/ppermute | solution.py:23
  264.0 31.6 %collective-permute-start.32 = (f32[1,256,1024]{2,1,0:T(8,128)}, f32[1,256,1024]{2,1,0:T(8,128)}, u32[]{:S(2)}, u32[]{:S(2)}) collective-permute-start(f32[1,256,1024]{2,1,0:T(8,128)} %get-tuple-element.22), channel_id=1, source_target_pairs={{0,4},{4,8},{8,12},{12,16},{16,20},{20,24},{24,28},{28,32},{32,36}... | collective-permute-start | bytes 3145736 | tf_op jit(solution)/shard_map/ppermute | solution.py:31
  269.7 18.7 %collective-permute-start.30 = (f32[2,1,1024]{2,1,0:T(1,128)S(1)}, f32[2,1,1024]{2,1,0:T(1,128)S(1)}, u32[]{:S(2)}, u32[]{:S(2)}) collective-permute-start(f32[2,1,1024]{2,1,0:T(1,128)S(1)} %get-tuple-element.25), channel_id=1, source_target_pairs={{1,0},{2,1},{3,2},{5,4},{6,5},{7,6},{9,8},{10,9},{11,10},{13,12},{... | collective-permute-start | bytes 24584 | tf_op jit(solution)/shard_map/ppermute | solution.py:23
  271.0 23.8 %collective-permute-start.31 = (f32[2,1,1024]{2,1,0:T(1,128)S(1)}, f32[2,1,1024]{2,1,0:T(1,128)S(1)}, u32[]{:S(2)}, u32[]{:S(2)}) collective-permute-start(f32[2,1,1024]{2,1,0:T(1,128)S(1)} %get-tuple-element.24), channel_id=1, source_target_pairs={{0,1},{1,2},{2,3},{4,5},{5,6},{6,7},{8,9},{9,10},{10,11},{12,13},{... | collective-permute-start | bytes 24584 | tf_op jit(solution)/shard_map/ppermute | solution.py:20
  277.3 36.3 %collective-permute-start.35 = (f32[1,256,1024]{2,1,0:T(8,128)}, f32[1,256,1024]{2,1,0:T(8,128)S(1)}, u32[]{:S(2)}, u32[]{:S(2)}) collective-permute-start(f32[1,256,1024]{2,1,0:T(8,128)} %get-tuple-element.11), channel_id=1, source_target_pairs={{0,32},{4,36},{8,40},{12,44},{16,48},{20,52},{24,56},{28,60},{32,6... | collective-permute-start | bytes 3145736 | tf_op jit(solution)/shard_map/ppermute | solution.py:31
  287.1 16.3 %collective-permute-start.33 = (f32[1,1,1024]{2,1,0:T(1,128)S(1)}, f32[1,1,1024]{2,1,0:T(1,128)S(1)}, u32[]{:S(2)}, u32[]{:S(2)}) collective-permute-start(f32[1,1,1024]{2,1,0:T(1,128)S(1)} %get-tuple-element.35), channel_id=1, source_target_pairs={{1,0},{2,1},{3,2},{5,4},{6,5},{7,6},{9,8},{10,9},{11,10},{13,12},{... | collective-permute-start | bytes 12296 | tf_op jit(solution)/shard_map/ppermute | solution.py:23
  288.4 15.0 %collective-permute-start.34 = (f32[1,1,1024]{2,1,0:T(1,128)S(1)}, f32[1,1,1024]{2,1,0:T(1,128)S(1)}, u32[]{:S(2)}, u32[]{:S(2)}) collective-permute-start(f32[1,1,1024]{2,1,0:T(1,128)S(1)} %get-tuple-element.34), channel_id=1, source_target_pairs={{0,1},{1,2},{2,3},{4,5},{5,6},{6,7},{8,9},{9,10},{10,11},{12,13},{... | collective-permute-start | bytes 12296 | tf_op jit(solution)/shard_map/ppermute | solution.py:20
  300.1 16.4 %collective-permute-start.38 = (f32[1,256,1024]{2,1,0:T(8,128)}, f32[1,256,1024]{2,1,0:T(8,128)}, u32[]{:S(2)}, u32[]{:S(2)}) collective-permute-start(f32[1,256,1024]{2,1,0:T(8,128)} %get-tuple-element.18), channel_id=1, source_target_pairs={{0,4},{4,8},{8,12},{12,16},{16,20},{20,24},{24,28},{28,32},{32,36}... | collective-permute-start | bytes 3145736 | tf_op jit(solution)/shard_map/ppermute | solution.py:31
  303.9 11.8 %collective-permute-start.36 = (f32[2,1,1024]{2,1,0:T(1,128)S(1)}, f32[2,1,1024]{2,1,0:T(1,128)S(1)}, u32[]{:S(2)}, u32[]{:S(2)}) collective-permute-start(f32[2,1,1024]{2,1,0:T(1,128)S(1)} %get-tuple-element.21), channel_id=1, source_target_pairs={{1,0},{2,1},{3,2},{5,4},{6,5},{7,6},{9,8},{10,9},{11,10},{13,12},{... | collective-permute-start | bytes 24584 | tf_op jit(solution)/shard_map/ppermute | solution.py:23
  305.2 10.5 %collective-permute-start.37 = (f32[2,1,1024]{2,1,0:T(1,128)S(1)}, f32[2,1,1024]{2,1,0:T(1,128)S(1)}, u32[]{:S(2)}, u32[]{:S(2)}) collective-permute-start(f32[2,1,1024]{2,1,0:T(1,128)S(1)} %get-tuple-element.20), channel_id=1, source_target_pairs={{0,1},{1,2},{2,3},{4,5},{5,6},{6,7},{8,9},{9,10},{10,11},{12,13},{... | collective-permute-start | bytes 24584 | tf_op jit(solution)/shard_map/ppermute | solution.py:20
  (22 other events, 174.3 us)
